TPU v7x, 512 devices: a 8x2x16 block of a 8x8x16 slice. The times are simulated.
512 devices in a mesh: job: 2 (over y), chain: 16 (over z), pair: 8 (over x), pno: 2 (over core).
Axes of the slice: x: 8, y: 2, z: 16, core: 2. Of those that a mesh axis runs over, the one named last changes fastest.
The devices are a block of a 8x8x16 slice.
Arguments:
- amplitudes: bfloat16 [1536, 128, 128], P(('job', 'chain', 'pair'), 'pno'), parts along dimension 0, may hold values from -4 to 4
- integrals: bfloat16 [1536, 128, 128], P(('job', 'chain', 'pair'), 'pno'), parts along dimension 0, may hold values from -6 to 6
- intersections: bfloat16 [1536, 32, 128, 128], P(('job', 'chain', 'pair')), parts along dimension 0, may hold values from -0.5 to 0.5
- coupling: float32 [1536, 32], P(('job', 'chain', 'pair')), parts along dimension 0, may hold values from -4 to 4
- pno_energies: float32 [1536, 128], P(('job', 'chain', 'pair')), parts along dimension 0, may hold values from 0.3 to 3
- pair_shift: float32 [1536], P(('job', 'chain', 'pair')), parts along dimension 0, may hold values from -1.5 to -0.3
- ranks: int32 [1536], P(('job', 'chain', 'pair')), parts along dimension 0, may hold values from 24 to 128
- neighbours: int32 [1536, 32], P(('job', 'chain', 'pair')), parts along dimension 0, may hold values from 0 to 767, as said below
Outputs:
- final_amplitudes: bfloat16 [1536, 128, 128], P(('job', 'chain', 'pair'), 'pno'), parts along dimension 0
- residual_norms: float32 [6], P('job'), parts along dimension 0
There are 2 independent parts, one for each index of `job`. A program takes and returns all parts, laid end to end along the dimension named above; each array names one. Nothing has to cross between parts.
Inputs may be any that keep to these rules, and one draw needn't show every extreme that they name: `neighbours`: every coupled pair of pair g lies in the fragment of g (pairs k * 48 to (k + 1) * 48 - 1 for k = g // 48) or in one of the two fragments beside it.
All inputs are finite; a program needn't handle non-finite values.
Results may differ from a plain program's by a relative error of at most 0.015.
Values may be sent and summed in bfloat16 or wider, within the bound.
No kernel may reach another device: no remote copies, remote signals or barrier semaphores. Data moves between devices by JAX's collectives and lax.ppermute only.
A program may use at most 64 MiB of HBM per device.

v0:
```python
import jax
import jax.numpy as jnp
from jax import lax
from jax.sharding import PartitionSpec as P

ITERS = 3


def laid_out(tiles, dim):
    tiles = jnp.moveaxis(tiles, 0, dim)
    shape = tiles.shape
    return tiles.reshape(*shape[:dim], shape[dim] * shape[dim + 1], *shape[dim + 2 :])


def copy_for_each(value, axis):
    copies = jnp.broadcast_to(value, (lax.axis_size(axis), *value.shape))
    return lax.all_to_all(copies, axis, split_axis=0, concat_axis=0, tiled=True)


def gathered_copies(value, axis, dim):
    return laid_out(copy_for_each(value, axis), dim)


def padded(cells, sides, width):
    for axis, dim in sides:
        count = lax.axis_size(axis)
        ends = count - 1
        head = lax.slice_in_dim(cells, 0, width, axis=dim)
        tail = lax.slice_in_dim(cells, cells.shape[dim] - width, cells.shape[dim], axis=dim)
        cells = jnp.concatenate(
            [
                lax.ppermute(tail, axis, [(i, (i + 1) % count) for i in range(ends)]),
                cells,
                lax.ppermute(head, axis, [((i + 1) % count, i) for i in range(ends)]),
            ],
            axis=dim,
        )
    return cells


def over_axes(value, axes):
    for axis in axes:
        value = lax.psum(value, axis)
    return value


def spread_amps(piece):
    whole_rows = gathered_copies(piece, "pno", 1)
    beside = padded(whole_rows, (("chain", 0),), whole_rows.shape[0])
    return lax.all_gather(beside, "pair", axis=0, tiled=True)


def per_device(
    amplitudes, integrals, intersections, coupling, pno_energies, pair_shift, ranks, neighbours
):
    count = amplitudes.shape[0]
    half = amplitudes.shape[1]
    width = amplitudes.shape[2]
    chain_pos = lax.axis_index("chain")
    first_row = lax.axis_index("pno") * half
    frag = count * lax.axis_size("pair")
    cells = frag * lax.axis_size("chain") * width * width
    columns = jnp.arange(width, dtype=jnp.int32)
    rows_here = first_row + jnp.arange(half, dtype=jnp.int32)
    live_cols = columns[None, :] < ranks[:, None]
    live_rows = rows_here[None, :] < ranks[:, None]
    mask = (live_rows[:, :, None] & live_cols[:, None, :]).astype(jnp.float32)
    energy_rows = lax.dynamic_slice_in_dim(pno_energies, first_row, half, 1)
    denom = energy_rows[:, :, None] + pno_energies[:, None, :] - pair_shift[:, None, None]
    over_rows = lax.dynamic_slice_in_dim(intersections, first_row, half, 2)
    own = (amplitudes.astype(jnp.float32) * mask).astype(jnp.bfloat16)
    ints = integrals.astype(jnp.float32)
    offset = neighbours // frag - chain_pos + 1
    within = neighbours % frag
    slots = within // count * (3 * count) + offset * count + within % count
    window = spread_amps(own)
    norms = []
    for step_no in range(ITERS):
        blocks = jnp.take(window, slots, axis=0)
        proj = jnp.einsum(
            "pnab,pnbc->pnac", over_rows, blocks, preferred_element_type=jnp.float32
        ).astype(jnp.bfloat16)
        terms = jnp.einsum(
            "pnac,pnbc->pnab", proj, intersections, preferred_element_type=jnp.float32
        )
        coupled = jnp.einsum("pn,pnab->pab", coupling, terms)
        own32 = own.astype(jnp.float32)
        resid = mask * (ints + coupled - denom * own32)
        delta = resid / denom
        more = step_no + 1 < ITERS
        squares = over_axes(jnp.sum(resid * resid), ("chain", "pair", "pno"))
        rms = jnp.sqrt(squares / cells)
        factor = 1.0 / (1.0 + rms)
        norms.append(rms)
        own = (own32 + delta * factor).astype(jnp.bfloat16)
        if more:
            window = spread_amps(own)
    return (own, jnp.stack(norms))


def solution(mesh):
    in_specs = (
        P(("job", "chain", "pair"), "pno", None),
        P(("job", "chain", "pair"), "pno", None),
        P(("job", "chain", "pair"), None, None, None),
        P(("job", "chain", "pair"), None),
        P(("job", "chain", "pair"), None),
        P(("job", "chain", "pair")),
        P(("job", "chain", "pair")),
        P(("job", "chain", "pair"), None),
    )
    out_specs = (P(("job", "chain", "pair"), "pno", None), P("job"))
    return jax.shard_map(
        per_device, mesh=mesh, in_specs=in_specs, out_specs=out_specs, check_vma=False
    )
```

profile of v0, /device:TPU:65, one launch (start us, length us, event | category | flops | bytes accessed | tf_op | source)
XLA Modules:
  0.0 529.5 jit_solution(2827774392820882856)
XLA Ops:
  9.8 45.0 %all_to_all.15 = bf16[2,6,64,128]{3,2,1,0:T(8,128)(2,1)S(1)} all-to-all(bf16[2,6,64,128]{3,2,1,0:T(8,128)(2,1)S(1)} %broadcast_in_dim.12), channel_id=1, replica_groups=mesh['job'=2,'chain'=16,'pair'=8,'pno'=2] {'pno'}, dimensions={0} | all-to-all | bytes 393216 | tf_op jit(solution)/shard_map/all_to_all | solution.py:17
  56.1 4.0 collective-permute-start
  66.3 58.9 %all-gather.4.cloned.1.call-done = bf16[144,128,128]{2,1,0:T(8,128)(2,1)} async-done(((bf16[18,128,128]{2,1,0:T(8,128)(2,1)}), bf16[144,128,128]{2,1,0:T(8,128)(2,1)}) %all-gather.4.cloned.1.call-update) | async-done | bytes 4718608 | tf_op jit(solution)/shard_map/all_gather | solution.py:50
  125.2 10.4 %gather_fusion = bf16[192,128,128]{2,1,0:T(8,128)(2,1)} fusion(bf16[144,128,128]{2,1,0:T(8,128)(2,1)} %all-gather.4.cloned.1.call-done, s32[1024]{0:T(1024)S(1)} %pad_clamp_fusion), kind=kCustom, calls=%fused_computation.clone | custom fusion | bytes 12583680 | tf_op jit(solution)/shard_map/jit(_take)/gather | solution.py:79
  135.6 10.9 %fusion.22 = bf16[6,32,64,128]{3,2,1,0:T(8,128)(2,1)} fusion(bf16[6,32,128,128]{3,2,1,0:T(8,128)(2,1)} %param.12, bf16[6,32,128,128]{3,2,1,0:T(8,128)(2,1)} %bitcast.29, pred[6,32]{1,0:T(8,128)(4,1)S(1)} %get-tuple-element.3, s32[]{:T(128)S(6)} %select_n.29), kind=kOutput, calls=%fused_computation.25 | convolution fusion | flops 810024960 | bytes 18874564 | tf_op jit(solution)/shard_map/pnac,pnbc->pnab/dot_general | solution.py:83
  151.0 25.8 %psum.63 = f32[]{:T(128)} all-reduce(f32[]{:T(128)} %multiply_reduce_fusion.2), channel_id=1, replica_groups=mesh['job'=2,'chain'=16,'pair'=8,'pno'=2] {'chain'}, use_global_device_ids=true, to_apply=%region_1.3 | all-reduce | flops 1 | bytes 8 | tf_op jit(solution)/shard_map/psum | solution.py:43
  176.7 12.7 %psum.64 = f32[]{:T(128)} all-reduce(f32[]{:T(128)} %psum.63), channel_id=1, replica_groups=mesh['job'=2,'chain'=16,'pair'=8,'pno'=2] {'pair'}, use_global_device_ids=true, to_apply=%region_2.4 | all-reduce | flops 1 | bytes 8 | tf_op jit(solution)/shard_map/psum | solution.py:43
  189.4 14.2 %psum.65 = f32[]{:T(128)} all-reduce(f32[]{:T(128)} %psum.64), channel_id=1, replica_groups=mesh['job'=2,'chain'=16,'pair'=8,'pno'=2] {'pno'}, use_global_device_ids=true, to_apply=%region_3.5 | all-reduce | flops 1 | bytes 8 | tf_op jit(solution)/shard_map/psum | solution.py:43
  204.6 3.9 all_to_all.16
  209.8 4.0 collective-permute-start.2
  218.6 65.3 %all-gather.6.cloned.1.call-done = bf16[144,128,128]{2,1,0:T(8,128)(2,1)} async-done(((bf16[18,128,128]{2,1,0:T(8,128)(2,1)}), bf16[144,128,128]{2,1,0:T(8,128)(2,1)}) %all-gather.6.cloned.1.call-update) | async-done | bytes 4718608 | tf_op jit(solution)/shard_map/all_gather | solution.py:50
  283.9 10.4 %gather_fusion.1 = bf16[192,128,128]{2,1,0:T(8,128)(2,1)} fusion(bf16[144,128,128]{2,1,0:T(8,128)(2,1)} %all-gather.6.cloned.1.call-done, s32[1024]{0:T(1024)S(1)} %pad_clamp_fusion), kind=kCustom, calls=%fused_computation.1.clone | custom fusion | bytes 12583680 | tf_op jit(solution)/shard_map/jit(_take)/gather | solution.py:79
  294.3 10.8 %fusion.20 = bf16[6,32,64,128]{3,2,1,0:T(8,128)(2,1)} fusion(bf16[6,32,128,128]{3,2,1,0:T(8,128)(2,1)} %param.12, bf16[6,32,128,128]{3,2,1,0:T(8,128)(2,1)} %bitcast.30, pred[6,32]{1,0:T(8,128)(4,1)S(1)} %get-tuple-element.3, s32[]{:T(128)S(6)} %select_n.29), kind=kOutput, calls=%fused_computation.23 | convolution fusion | flops 810024960 | bytes 18874564 | tf_op jit(solution)/shard_map/pnac,pnbc->pnab/dot_general | solution.py:83
  309.6 25.8 %psum.66 = f32[]{:T(128)} all-reduce(f32[]{:T(128)} %multiply_reduce_fusion.1), channel_id=1, replica_groups=mesh['job'=2,'chain'=16,'pair'=8,'pno'=2] {'chain'}, use_global_device_ids=true, to_apply=%region_5.7 | all-reduce | flops 1 | bytes 8 | tf_op jit(solution)/shard_map/psum | solution.py:43
  335.4 12.7 %psum.67 = f32[]{:T(128)} all-reduce(f32[]{:T(128)} %psum.66), channel_id=1, replica_groups=mesh['job'=2,'chain'=16,'pair'=8,'pno'=2] {'pair'}, use_global_device_ids=true, to_apply=%region_6.8 | all-reduce | flops 1 | bytes 8 | tf_op jit(solution)/shard_map/psum | solution.py:43
  348.0 14.2 %psum.68 = f32[]{:T(128)} all-reduce(f32[]{:T(128)} %psum.67), channel_id=1, replica_groups=mesh['job'=2,'chain'=16,'pair'=8,'pno'=2] {'pno'}, use_global_device_ids=true, to_apply=%region_7.9 | all-reduce | flops 1 | bytes 8 | tf_op jit(solution)/shard_map/psum | solution.py:43
  363.2 3.9 all_to_all.17
  368.4 4.3 collective-permute-start.4
  377.0 65.5 %all-gather.8.cloned.1.call-done = bf16[144,128,128]{2,1,0:T(8,128)(2,1)} async-done(((bf16[18,128,128]{2,1,0:T(8,128)(2,1)}), bf16[144,128,128]{2,1,0:T(8,128)(2,1)}) %all-gather.8.cloned.1.call-update) | async-done | bytes 4718608 | tf_op jit(solution)/shard_map/all_gather | solution.py:50
  442.5 10.4 %gather_fusion.2 = bf16[192,128,128]{2,1,0:T(8,128)(2,1)} fusion(bf16[144,128,128]{2,1,0:T(8,128)(2,1)} %all-gather.8.cloned.1.call-done, s32[1024]{0:T(1024)S(1)} %pad_clamp_fusion), kind=kCustom, calls=%fused_computation.2.clone | custom fusion | bytes 12583680 | tf_op jit(solution)/shard_map/jit(_take)/gather | solution.py:79
  452.9 10.8 %fusion.18 = bf16[6,32,64,128]{3,2,1,0:T(8,128)(2,1)} fusion(bf16[6,32,128,128]{3,2,1,0:T(8,128)(2,1)} %param.12, bf16[6,32,128,128]{3,2,1,0:T(8,128)(2,1)} %bitcast.28, pred[6,32]{1,0:T(8,128)(4,1)S(1)} %get-tuple-element.3, s32[]{:T(128)S(6)} %select_n.29), kind=kOutput, calls=%fused_computation.21 | convolution fusion | flops 810024960 | bytes 18874564 | tf_op jit(solution)/shard_map/pnac,pnbc->pnab/dot_general | solution.py:83
  468.2 26.0 %psum.69 = f32[]{:T(128)} all-reduce(f32[]{:T(128)} %multiply_reduce_fusion), channel_id=1, replica_groups=mesh['job'=2,'chain'=16,'pair'=8,'pno'=2] {'chain'}, use_global_device_ids=true, to_apply=%region_9.11 | all-reduce | flops 1 | bytes 8 | tf_op jit(solution)/shard_map/psum | solution.py:43
  494.2 12.5 %psum.70 = f32[]{:T(128)} all-reduce(f32[]{:T(128)} %psum.69), channel_id=1, replica_groups=mesh['job'=2,'chain'=16,'pair'=8,'pno'=2] {'pair'}, use_global_device_ids=true, to_apply=%region_10.12 | all-reduce | flops 1 | bytes 8 | tf_op jit(solution)/shard_map/psum | solution.py:43
  506.7 14.2 %psum.71 = f32[]{:T(128)} all-reduce(f32[]{:T(128)} %psum.70), channel_id=1, replica_groups=mesh['job'=2,'chain'=16,'pair'=8,'pno'=2] {'pno'}, use_global_device_ids=true, to_apply=%region_11.13 | all-reduce | flops 1 | bytes 8 | tf_op jit(solution)/shard_map/psum | solution.py:43
  (52 shorter events, 37.1 us)
Async XLA Ops:
  7.2 139.3 %copy-start = (f32[6,32]{1,0:T(8,128)S(1)}, f32[6,32]{1,0:T(8,128)}, u32[]{:S(2)}) copy-start(f32[6,32]{1,0:T(8,128)} %param.13) | copy-start | bytes 2308
  7.2 118.0 %all-gather.4.cloned.1.call-start = ((), (), s32[]{:S(2)}) async-start(), calls=%async_computation.3 | async-start | bytes 5308416 | tf_op jit(solution)/shard_map/all_gather | solution.py:50
  54.8 8.0 %collective-permute-start.1 = (bf16[6,128,128]{2,1,0:T(8,128)(2,1)S(1)}, bf16[6,128,128]{2,1,0:T(8,128)(2,1)S(1)}, u32[]{:S(2)}, u32[]{:S(2)}) collective-permute-start(bf16[6,128,128]{2,1,0:T(8,128)(2,1)S(1)} %bitcast.31), channel_id=1, source_target_pairs={{16,0},{32,16},{48,32},{64,48},{80,64},{96,80},{112,96},{128,112},... | collective-permute-start | bytes 589832 | tf_op jit(solution)/shard_map/ppermute | solution.py:34
  56.1 7.6 %collective-permute-start = (bf16[6,128,128]{2,1,0:T(8,128)(2,1)S(1)}, bf16[6,128,128]{2,1,0:T(8,128)(2,1)S(1)}, u32[]{:S(2)}, u32[]{:S(2)}) collective-permute-start(bf16[6,128,128]{2,1,0:T(8,128)(2,1)S(1)} %bitcast.32), channel_id=1, source_target_pairs={{0,16},{16,32},{32,48},{48,64},{64,80},{80,96},{96,112},{112,128},... | collective-permute-start | bytes 589832 | tf_op jit(solution)/shard_map/ppermute | solution.py:32
  64.7 219.2 %all-gather.6.cloned.1.call-start = ((), (), s32[]{:S(2)}) async-start(), calls=%async_computation.4 | async-start | bytes 5308416 | tf_op jit(solution)/shard_map/all_gather | solution.py:50
  135.6 14.6 %copy-start.1 = (bf16[6,64,128]{2,1,0:T(8,128)(2,1)S(1)}, bf16[6,64,128]{2,1,0:T(8,128)(2,1)}, u32[]{:S(2)}) copy-start(bf16[6,64,128]{2,1,0:T(8,128)(2,1)} %param.11) | copy-start | bytes 294916
  135.6 14.6 %copy-start.2 = (bf16[6,64,128]{2,1,0:T(8,128)(2,1)S(1)}, bf16[6,64,128]{2,1,0:T(8,128)(2,1)}, u32[]{:S(2)}) copy-start(bf16[6,64,128]{2,1,0:T(8,128)(2,1)} %param.10) | copy-start | bytes 294916
  135.6 14.6 %copy-start.3 = (f32[6,128]{1,0:T(8,128)S(1)}, f32[6,128]{1,0:T(8,128)}, u32[]{:S(2)}) copy-start(f32[6,128]{1,0:T(8,128)} %param.14) | copy-start | bytes 9220
  135.6 14.6 %copy-start.4 = (f32[6]{0:T(128)S(1)}, f32[6]{0:T(128)}, u32[]{:S(2)}) copy-start(f32[6]{0:T(128)} %param.15) | copy-start | bytes 76
  208.5 8.0 %collective-permute-start.3 = (bf16[6,128,128]{2,1,0:T(8,128)(2,1)S(1)}, bf16[6,128,128]{2,1,0:T(8,128)(2,1)S(1)}, u32[]{:S(2)}, u32[]{:S(2)}) collective-permute-start(bf16[6,128,128]{2,1,0:T(8,128)(2,1)S(1)} %bitcast.34), channel_id=1, source_target_pairs={{16,0},{32,16},{48,32},{64,48},{80,64},{96,80},{112,96},{128,112},... | collective-permute-start | bytes 589832 | tf_op jit(solution)/shard_map/ppermute | solution.py:34
  209.8 7.6 %collective-permute-start.2 = (bf16[6,128,128]{2,1,0:T(8,128)(2,1)S(1)}, bf16[6,128,128]{2,1,0:T(8,128)(2,1)S(1)}, u32[]{:S(2)}, u32[]{:S(2)}) collective-permute-start(bf16[6,128,128]{2,1,0:T(8,128)(2,1)S(1)} %bitcast.35), channel_id=1, source_target_pairs={{0,16},{16,32},{32,48},{48,64},{64,80},{80,96},{96,112},{112,128},... | collective-permute-start | bytes 589832 | tf_op jit(solution)/shard_map/ppermute | solution.py:32
  218.4 224.2 %all-gather.8.cloned.1.call-start = ((), (), s32[]{:S(2)}) async-start(), calls=%async_computation.5 | async-start | bytes 5308416 | tf_op jit(solution)/shard_map/all_gather | solution.py:50
  367.1 8.0 %collective-permute-start.5 = (bf16[6,128,128]{2,1,0:T(8,128)(2,1)S(1)}, bf16[6,128,128]{2,1,0:T(8,128)(2,1)S(1)}, u32[]{:S(2)}, u32[]{:S(2)}) collective-permute-start(bf16[6,128,128]{2,1,0:T(8,128)(2,1)S(1)} %bitcast.37), channel_id=1, source_target_pairs={{16,0},{32,16},{48,32},{64,48},{80,64},{96,80},{112,96},{128,112},... | collective-permute-start | bytes 589832 | tf_op jit(solution)/shard_map/ppermute | solution.py:34
  368.4 7.6 %collective-permute-start.4 = (bf16[6,128,128]{2,1,0:T(8,128)(2,1)S(1)}, bf16[6,128,128]{2,1,0:T(8,128)(2,1)S(1)}, u32[]{:S(2)}, u32[]{:S(2)}) collective-permute-start(bf16[6,128,128]{2,1,0:T(8,128)(2,1)S(1)} %bitcast.38), channel_id=1, source_target_pairs={{0,16},{16,32},{32,48},{48,64},{64,80},{80,96},{96,112},{112,128},... | collective-permute-start | bytes 589832 | tf_op jit(solution)/shard_map/ppermute | solution.py:32
Sparse Core Ops, SparseCore 0:
  64.8 60.3 all-gather.3
  218.5 65.3 all-gather.5
  377.1 65.3 all-gather.7
where the time goes:
time: 530 us
  blocking collectives  211 us (40%)
  waiting for transfers between devices  200 us (38%)
  matrix products  43.6 us (8%)
  local copies, waits for them, and re-layouts  32.2 us (6%)
  starting transfers between devices  16.6 us (3%)
  between operations  16.1 us (3%)
  other arithmetic  9.94 us (2%)
    all_gather x3, waiting for transfers between devices, spread_amps(): return lax.all_gather(beside, 'pair', axis=0, tiled=True)  190 us
    psum x9, blocking collectives, over_axes(): value = lax.psum(value, axis)  158 us
    all_to_all x3, blocking collectives, copy_for_each(): return lax.all_to_all(copies, axis, split_axis=0, concat_axis=0, tiled=True)  52.8 us
    dot_general x3, matrix products, per_device(): jnp.einsum('pnac,pnbc->pnab', proj, intersections, preferred_element_type...  32.5 us
    gather x3, local copies, waits for them, and re-layouts, per_device(): blocks = jnp.take(window, slots, axis=0)  31.2 us
    ppermute x3, starting transfers between devices, padded(): lax.ppermute(tail, axis, [(i, (i + 1) % count) for i in range(ends)])  12.4 us
    dot_general x3, matrix products, per_device(): coupled = jnp.einsum('pn,pnab->pab', coupling, terms)  11.2 us
  transfers between devices with their start and end apart: 9, of which 9 were waited for; matrix products, arithmetic and copies ran while one was open for 0% of the time, Pallas kernels for 0%

commit v1 on v0

--- a/solution.py
+++ b/solution.py
@@ -4,6 +4,11 @@
 from jax.sharding import PartitionSpec as P
 
 ITERS = 3
+
+
+def tiled_gather(x, axis, dim):
+    copies = jnp.concatenate([x] * lax.axis_size(axis), axis=dim)
+    return lax.all_to_all(copies, axis, dim, dim, tiled=True)
 
 
 def laid_out(tiles, dim):
@@ -47,7 +52,7 @@
 def spread_amps(piece):
     whole_rows = gathered_copies(piece, "pno", 1)
     beside = padded(whole_rows, (("chain", 0),), whole_rows.shape[0])
-    return lax.all_gather(beside, "pair", axis=0, tiled=True)
+    return tiled_gather(beside, "pair", 0)
 
 
 def per_device(

time: 530 us -> 669 us (1.26)
  blocking collectives: 211 us -> 424 us
  waiting for transfers between devices: 200 us -> 126 us
  local copies, waits for them, and re-layouts: 32.2 us -> 49.3 us
  between operations: 16.1 us -> 3.35 us
    all_to_all x0 -> x2, blocking collectives: none -> 217 us  [tiled_gather(): return lax.all_to_all(copies, axis, dim, dim, tiled=True)]
    all_gather x3 -> x0, waiting for transfers between devices: 190 us -> none  [spread_amps(): return lax.all_gather(beside, 'pair', axis=0, tiled=True)]
    all_to_all x0 -> x1, waiting for transfers between devices: none -> 108 us  [tiled_gather(): return lax.all_to_all(copies, axis, dim, dim, tiled=True)]
    unnamed x10 -> x81, local copies, waits for them, and re-layouts: 0.02 us -> 17.1 us
  transfers between devices with their start and end apart: 9 -> 7, of which waited for: 9 -> 7; matrix products, arithmetic and copies ran while one was open for 0% -> 0% of each run, Pallas kernels for 0% -> 0%
where the time goes in v1:
time: 669 us; the launch traced here: 668 us
  blocking collectives  424 us (63%)
  waiting for transfers between devices  126 us (19%)
  local copies, waits for them, and re-layouts  49.3 us (7%)
  matrix products  43.6 us (7%)
  starting transfers between devices  14.6 us (2%)
    all_to_all x2, blocking collectives, tiled_gather(): return lax.all_to_all(copies, axis, dim, dim, tiled=True)  217 us
    psum x9, blocking collectives, over_axes(): value = lax.psum(value, axis)  155 us
    all_to_all x1, waiting for transfers between devices, tiled_gather(): return lax.all_to_all(copies, axis, dim, dim, tiled=True)  108 us
    all_to_all x3, blocking collectives, copy_for_each(): return lax.all_to_all(copies, axis, split_axis=0, concat_axis=0, tiled=True)  52.8 us
    dot_general x3, matrix products, per_device(): jnp.einsum('pnac,pnbc->pnab', proj, intersections, preferred_element_type...  32.4 us
    gather x3, local copies, waits for them, and re-layouts, per_device(): blocks = jnp.take(window, slots, axis=0)  31.2 us
    unnamed x81, local copies, waits for them, and re-layouts  17.1 us
  transfers between devices with their start and end apart: 7, of which 7 were waited for; matrix products, arithmetic and copies ran while one was open for 0% of the time, Pallas kernels for 0%

profile of v1, /device:TPU:65, one launch (start us, length us, event | category | flops | bytes accessed | tf_op | source)
XLA Modules:
  0.0 667.6 jit_solution(1467421379075168891)
XLA Ops:
  3.2 45.0 %all_to_all.30 = bf16[2,6,64,128]{3,2,1,0:T(8,128)(2,1)S(1)} all-to-all(bf16[2,6,64,128]{3,2,1,0:T(8,128)(2,1)S(1)} %broadcast_in_dim.12), channel_id=1, replica_groups=mesh['job'=2,'chain'=16,'pair'=8,'pno'=2] {'pno'}, dimensions={0} | all-to-all | bytes 393216 | tf_op jit(solution)/shard_map/all_to_all | solution.py:22
  72.6 4.9 all-to-all-start.1
  77.8 107.8 %all-to-all-done.1 = bf16[144,128,128]{2,1,0:T(8,128)(2,1)} async-done(((bf16[144,128,128]{2,1,0:T(8,128)(2,1)}), bf16[144,128,128]{2,1,0:T(8,128)(2,1)}, u32[]{:S(2)}, u32[]{:S(2)}) %all-to-all-start.1) | async-done | bytes 4718624 | tf_op jit(solution)/shard_map/all_to_all | solution.py:11
  185.6 10.4 %gather_fusion = bf16[192,128,128]{2,1,0:T(8,128)(2,1)} fusion(bf16[144,128,128]{2,1,0:T(8,128)(2,1)} %all-to-all-done.1, s32[1024]{0:T(1024)S(1)} %pad_clamp_fusion), kind=kCustom, calls=%fused_computation.clone | custom fusion | bytes 12583680 | tf_op jit(solution)/shard_map/jit(_take)/gather | solution.py:84
  196.0 10.8 %fusion.22 = bf16[6,32,64,128]{3,2,1,0:T(8,128)(2,1)} fusion(bf16[6,32,128,128]{3,2,1,0:T(8,128)(2,1)} %param.12, bf16[6,32,128,128]{3,2,1,0:T(8,128)(2,1)} %bitcast.59, pred[6,32]{1,0:T(8,128)(4,1)S(1)} %get-tuple-element.3, s32[]{:T(128)S(6)} %select_n.29), kind=kOutput, calls=%fused_computation.25 | convolution fusion | flops 810024960 | bytes 18874564 | tf_op jit(solution)/shard_map/pnac,pnbc->pnab/dot_general | solution.py:88
  211.3 25.0 %psum.63 = f32[]{:T(128)} all-reduce(f32[]{:T(128)} %multiply_reduce_fusion.2), channel_id=1, replica_groups=mesh['job'=2,'chain'=16,'pair'=8,'pno'=2] {'chain'}, use_global_device_ids=true, to_apply=%region_1.3 | all-reduce | flops 1 | bytes 8 | tf_op jit(solution)/shard_map/psum | solution.py:48
  236.3 11.4 %psum.64 = f32[]{:T(128)} all-reduce(f32[]{:T(128)} %psum.63), channel_id=1, replica_groups=mesh['job'=2,'chain'=16,'pair'=8,'pno'=2] {'pair'}, use_global_device_ids=true, to_apply=%region_2.4 | all-reduce | flops 1 | bytes 8 | tf_op jit(solution)/shard_map/psum | solution.py:48
  247.7 14.2 %psum.65 = f32[]{:T(128)} all-reduce(f32[]{:T(128)} %psum.64), channel_id=1, replica_groups=mesh['job'=2,'chain'=16,'pair'=8,'pno'=2] {'pno'}, use_global_device_ids=true, to_apply=%region_3.5 | all-reduce | flops 1 | bytes 8 | tf_op jit(solution)/shard_map/psum | solution.py:48
  262.9 3.9 all_to_all.31
  273.2 3.8 collective-permute-done.3
  277.8 108.2 %all_to_all.32 = bf16[144,128,128]{2,1,0:T(8,128)(2,1)} all-to-all(bf16[144,128,128]{2,1,0:T(8,128)(2,1)S(1)} %constant_dynamic-update-slice_fusion.24), channel_id=1, replica_groups=mesh['job'=2,'chain'=16,'pair'=8,'pno'=2] {'pair'}, dimensions={0} | all-to-all | bytes 9437184 | tf_op jit(solution)/shard_map/all_to_all | solution.py:11
  386.0 10.4 %gather_fusion.1 = bf16[192,128,128]{2,1,0:T(8,128)(2,1)} fusion(bf16[144,128,128]{2,1,0:T(8,128)(2,1)} %all_to_all.32, s32[1024]{0:T(1024)S(1)} %pad_clamp_fusion), kind=kCustom, calls=%fused_computation.1.clone | custom fusion | bytes 12583680 | tf_op jit(solution)/shard_map/jit(_take)/gather | solution.py:84
  396.4 10.8 %fusion.20 = bf16[6,32,64,128]{3,2,1,0:T(8,128)(2,1)} fusion(bf16[6,32,128,128]{3,2,1,0:T(8,128)(2,1)} %param.12, bf16[6,32,128,128]{3,2,1,0:T(8,128)(2,1)} %bitcast.60, pred[6,32]{1,0:T(8,128)(4,1)S(1)} %get-tuple-element.3, s32[]{:T(128)S(6)} %select_n.29), kind=kOutput, calls=%fused_computation.23 | convolution fusion | flops 810024960 | bytes 18874564 | tf_op jit(solution)/shard_map/pnac,pnbc->pnab/dot_general | solution.py:88
  411.7 22.4 %psum.66 = f32[]{:T(128)} all-reduce(f32[]{:T(128)} %multiply_reduce_fusion.1), channel_id=1, replica_groups=mesh['job'=2,'chain'=16,'pair'=8,'pno'=2] {'chain'}, use_global_device_ids=true, to_apply=%region_5.7 | all-reduce | flops 1 | bytes 8 | tf_op jit(solution)/shard_map/psum | solution.py:48
  434.1 12.0 %psum.67 = f32[]{:T(128)} all-reduce(f32[]{:T(128)} %psum.66), channel_id=1, replica_groups=mesh['job'=2,'chain'=16,'pair'=8,'pno'=2] {'pair'}, use_global_device_ids=true, to_apply=%region_6.8 | all-reduce | flops 1 | bytes 8 | tf_op jit(solution)/shard_map/psum | solution.py:48
  446.1 16.6 %psum.68 = f32[]{:T(128)} all-reduce(f32[]{:T(128)} %psum.67), channel_id=1, replica_groups=mesh['job'=2,'chain'=16,'pair'=8,'pno'=2] {'pno'}, use_global_device_ids=true, to_apply=%region_7.9 | all-reduce | flops 1 | bytes 8 | tf_op jit(solution)/shard_map/psum | solution.py:48
  463.7 3.9 all_to_all.33
  473.5 3.8 collective-permute-done.5
  478.1 108.3 %all_to_all.34 = bf16[144,128,128]{2,1,0:T(8,128)(2,1)} all-to-all(bf16[144,128,128]{2,1,0:T(8,128)(2,1)S(1)} %constant_dynamic-update-slice_fusion.48), channel_id=1, replica_groups=mesh['job'=2,'chain'=16,'pair'=8,'pno'=2] {'pair'}, dimensions={0} | all-to-all | bytes 9437184 | tf_op jit(solution)/shard_map/all_to_all | solution.py:11
  586.4 10.4 %gather_fusion.2 = bf16[192,128,128]{2,1,0:T(8,128)(2,1)} fusion(bf16[144,128,128]{2,1,0:T(8,128)(2,1)} %all_to_all.34, s32[1024]{0:T(1024)S(1)} %pad_clamp_fusion), kind=kCustom, calls=%fused_computation.2.clone | custom fusion | bytes 12583680 | tf_op jit(solution)/shard_map/jit(_take)/gather | solution.py:84
  596.8 10.8 %fusion.18 = bf16[6,32,64,128]{3,2,1,0:T(8,128)(2,1)} fusion(bf16[6,32,128,128]{3,2,1,0:T(8,128)(2,1)} %param.12, bf16[6,32,128,128]{3,2,1,0:T(8,128)(2,1)} %bitcast.58, pred[6,32]{1,0:T(8,128)(4,1)S(1)} %get-tuple-element.3, s32[]{:T(128)S(6)} %select_n.29), kind=kOutput, calls=%fused_computation.21 | convolution fusion | flops 810024960 | bytes 18874564 | tf_op jit(solution)/shard_map/pnac,pnbc->pnab/dot_general | solution.py:88
  612.1 24.7 %psum.69 = f32[]{:T(128)} all-reduce(f32[]{:T(128)} %multiply_reduce_fusion), channel_id=1, replica_groups=mesh['job'=2,'chain'=16,'pair'=8,'pno'=2] {'chain'}, use_global_device_ids=true, to_apply=%region_9.11 | all-reduce | flops 1 | bytes 8 | tf_op jit(solution)/shard_map/psum | solution.py:48
  636.8 12.1 %psum.70 = f32[]{:T(128)} all-reduce(f32[]{:T(128)} %psum.69), channel_id=1, replica_groups=mesh['job'=2,'chain'=16,'pair'=8,'pno'=2] {'pair'}, use_global_device_ids=true, to_apply=%region_10.12 | all-reduce | flops 1 | bytes 8 | tf_op jit(solution)/shard_map/psum | solution.py:48
  648.9 16.6 %psum.71 = f32[]{:T(128)} all-reduce(f32[]{:T(128)} %psum.70), channel_id=1, replica_groups=mesh['job'=2,'chain'=16,'pair'=8,'pno'=2] {'pno'}, use_global_device_ids=true, to_apply=%region_11.13 | all-reduce | flops 1 | bytes 8 | tf_op jit(solution)/shard_map/psum | solution.py:48
  (118 shorter events, 56.0 us)
Async XLA Ops:
  0.6 206.2 %copy-start = (f32[6,32]{1,0:T(8,128)S(1)}, f32[6,32]{1,0:T(8,128)}, u32[]{:S(2)}) copy-start(f32[6,32]{1,0:T(8,128)} %param.13) | copy-start | bytes 2308
  48.2 5.5 collective-permute-start
  49.5 8.0 %collective-permute-start.1 = (bf16[6,128,128]{2,1,0:T(8,128)(2,1)S(1)}, bf16[6,128,128]{2,1,0:T(8,128)(2,1)S(1)}, u32[]{:S(2)}, u32[]{:S(2)}) collective-permute-start(bf16[6,128,128]{2,1,0:T(8,128)(2,1)S(1)} %bitcast.29), channel_id=1, source_target_pairs={{16,0},{32,16},{48,32},{64,48},{80,64},{96,80},{112,96},{128,112},... | collective-permute-start | bytes 589832 | tf_op jit(solution)/shard_map/ppermute | solution.py:39
  72.6 4.9 copy-start.5
  72.6 5.1 copy-start.3
  72.6 112.9 %all-to-all-start.1 = ((bf16[144,128,128]{2,1,0:T(8,128)(2,1)}), bf16[144,128,128]{2,1,0:T(8,128)(2,1)}, u32[]{:S(2)}, u32[]{:S(2)}) async-start(bf16[144,128,128]{2,1,0:T(8,128)(2,1)} %constant_dynamic-update-slice_fusion), calls=%async_computation.1 | async-start | bytes 9437184 | tf_op jit(solution)/shard_map/all_to_all | solution.py:11
  196.0 14.6 %copy-start.1 = (bf16[6,64,128]{2,1,0:T(8,128)(2,1)S(1)}, bf16[6,64,128]{2,1,0:T(8,128)(2,1)}, u32[]{:S(2)}) copy-start(bf16[6,64,128]{2,1,0:T(8,128)(2,1)} %param.11) | copy-start | bytes 294916
  196.0 14.6 %copy-start.2 = (bf16[6,64,128]{2,1,0:T(8,128)(2,1)S(1)}, bf16[6,64,128]{2,1,0:T(8,128)(2,1)}, u32[]{:S(2)}) copy-start(bf16[6,64,128]{2,1,0:T(8,128)(2,1)} %param.10) | copy-start | bytes 294916
  196.0 14.6 %copy-start.4 = (f32[6]{0:T(128)S(1)}, f32[6]{0:T(128)}, u32[]{:S(2)}) copy-start(f32[6]{0:T(128)} %param.15) | copy-start | bytes 76
  266.8 6.4 collective-permute-start.2
  269.3 7.7 %collective-permute-start.3 = (bf16[6,128,128]{2,1,0:T(8,128)(2,1)S(1)}, bf16[6,128,128]{2,1,0:T(8,128)(2,1)S(1)}, u32[]{:S(2)}, u32[]{:S(2)}) collective-permute-start(bf16[6,128,128]{2,1,0:T(8,128)(2,1)S(1)} %bitcast.39), channel_id=1, source_target_pairs={{16,0},{32,16},{48,32},{64,48},{80,64},{96,80},{112,96},{128,112},... | collective-permute-start | bytes 589832 | tf_op jit(solution)/shard_map/ppermute | solution.py:39
  467.6 5.8 collective-permute-start.4
  469.5 7.7 %collective-permute-start.5 = (bf16[6,128,128]{2,1,0:T(8,128)(2,1)S(1)}, bf16[6,128,128]{2,1,0:T(8,128)(2,1)S(1)}, u32[]{:S(2)}, u32[]{:S(2)}) collective-permute-start(bf16[6,128,128]{2,1,0:T(8,128)(2,1)S(1)} %bitcast.49), channel_id=1, source_target_pairs={{16,0},{32,16},{48,32},{64,48},{80,64},{96,80},{112,96},{128,112},... | collective-permute-start | bytes 589832 | tf_op jit(solution)/shard_map/ppermute | solution.py:39
